TPU v7x, 32 devices: a whole 2x2x4 slice. The times are simulated.
32 devices in a mesh: row: 4 (over x, core), col: 8 (over z, y).
Axes of the slice: x: 2, y: 2, z: 4, core: 2. Of those that a mesh axis runs over, the one named last changes fastest.
Arguments:
- left_factor: bfloat16 [4096, 2048], P('row', 'col'), may hold values from -6 to 6
- right_factor: bfloat16 [2048, 8192], P('row', 'col'), may hold values from -0.125 to 0.125
- matrix: float32 [4096, 8192], P('row', 'col'), may hold values from -6 to 6
- pivot_scale: float32 [2048], replicated, may hold values from 0.25 to 1.75
Outputs:
- updated: float32 [4096, 8192], P('row', 'col')
All inputs are finite; a program needn't handle non-finite values.
Results may differ from a plain program's by a relative error of at most 0.0003.
Values may be sent and summed in bfloat16 or wider, within the bound.
A program may use at most 128 MiB of HBM per device.

v0:
```python
import jax
import jax.numpy as jnp
from jax import lax
from jax.sharding import PartitionSpec as P


def taken_in(shard, axis, dim, absorb, state):
    everything = jax.tree.map(lambda a: lax.all_gather(a, axis, axis=dim, tiled=True), shard)
    return absorb(state, everything, jnp.int32(0))


def join_panel(carry, left_panel, right_panel):
    return carry + jnp.dot(left_panel, right_panel, preferred_element_type=jnp.float32)


def per_device(left_factor, right_factor, matrix, pivot_scale):
    share = left_factor.shape[1]
    part_scale = lax.dynamic_slice_in_dim(pivot_scale, lax.axis_index("col") * share, share)
    scaled_left = (left_factor.astype(jnp.float32) * part_scale).astype(jnp.bfloat16)
    begin = jnp.zeros((left_factor.shape[0], right_factor.shape[1]), jnp.float32)
    left_line = lax.all_gather(scaled_left, "col", axis=1, tiled=True)

    def take_rows(carry, piece, start):
        left_piece = lax.dynamic_slice_in_dim(left_line, start, piece.shape[0], axis=1)
        return join_panel(carry, left_piece, piece)

    total = taken_in(right_factor, "row", 0, take_rows, begin)
    updated = matrix - total
    row_power = lax.psum(jnp.sum(updated * updated, axis=1), "col")
    updated = (
        updated * lax.rsqrt(row_power / (updated.shape[1] * lax.axis_size("col")) + 1e-06)[:, None]
    )
    return updated


def solution(mesh):
    in_specs = (P("row", "col"), P("row", "col"), P("row", "col"), P())
    out_specs = P("row", "col")
    return jax.shard_map(
        per_device, mesh=mesh, in_specs=in_specs, out_specs=out_specs, check_vma=False
    )
```

profile of v0, /device:TPU:0, one launch (start us, length us, event | category | flops | bytes accessed | tf_op | source)
XLA Modules:
  0.0 169.9 jit_solution(15891152812098854044)
XLA Ops:
  6.5 0.0 all-gather.5.cloned.1.call-start
  6.5 0.7 all-gather.5.cloned.1.call-update
  7.3 0.0 all-gather.3.cloned.1.call-start
  7.3 0.8 dynamic_slice.3
  8.1 2.0 %multiply_convert_fusion = bf16[1024,256]{1,0:T(8,128)(2,1)} fusion(bf16[1024,256]{1,0:T(8,128)(2,1)} %param.4, f32[256]{0:T(256)S(1)} %dynamic_slice.3), kind=kLoop, calls=%fused_computation.3 | loop fusion | flops 786432 | bytes 1049600 | tf_op jit(solution)/shard_map/convert_element_type | solution.py:19
  10.1 0.0 all-gather.3.cloned.1.call-update
  10.1 5.3 %copy.5 = f32[1024,1024]{0,1:T(8,128)} copy(f32[1024,1024]{1,0:T(8,128)} %param.6) | data formatting | bytes 8388608 | tf_op args[2]
  15.4 30.7 %all-gather.5.cloned.1.call-done = bf16[2048,1024]{1,0:T(8,128)(2,1)} async-done(((bf16[512,1024]{1,0:T(8,128)(2,1)}), bf16[2048,1024]{1,0:T(8,128)(2,1)}) %all-gather.5.cloned.1.call-update) | async-done | bytes 4194320 | tf_op jit(solution)/shard_map/all_gather | solution.py:8
  46.1 76.7 %all-gather.3.cloned.1.call-done = bf16[1024,2048]{1,0:T(8,128)(2,1)} async-done(((bf16[1024,256]{1,0:T(8,128)(2,1)}), bf16[1024,2048]{1,0:T(8,128)(2,1)}) %all-gather.3.cloned.1.call-update) | async-done | bytes 4194320 | tf_op jit(solution)/shard_map/all_gather | solution.py:21
  122.8 11.3 %multiply_reduce_fusion = (f32[1024]{0:T(1024)S(1)}, f32[1024,1024]{0,1:T(8,128)}) fusion(f32[1024,1024]{0,1:T(8,128)} %copy.5, bf16[1024,2048]{1,0:T(8,128)(2,1)} %all-gather.3.cloned.1.call-done, bf16[2048,1024]{1,0:T(8,128)(2,1)} %all-gather.5.cloned.1.call-done), kind=kOutput, calls=%fused_computation | convolution fusion | flops 4298112000 | bytes 16781312 | tf_op jit(solution)/shard_map/dot_general | solution.py:13
  134.1 18.6 %psum.7 = f32[1024]{0:T(1024)S(1)} all-reduce(f32[1024]{0:T(1024)S(1)} %get-tuple-element.5), channel_id=1, replica_groups=mesh['row'=4,'col'=8] {'col'}, use_global_device_ids=true, to_apply=%region_1.0 | all-reduce | flops 1024 | bytes 8192 | tf_op jit(solution)/shard_map/psum | solution.py:29
  152.7 5.0 %broadcast_multiply_fusion = f32[1024,1024]{0,1:T(8,128)} fusion(f32[1024,1024]{0,1:T(8,128)} %get-tuple-element.6, f32[1024]{0:T(1024)S(1)} %add_rsqrt_fusion), kind=kLoop, calls=%fused_computation.1 | loop fusion | flops 1048576 | bytes 8392704 | tf_op jit(solution)/shard_map/mul | solution.py:31
  157.7 5.3 %copy.6 = f32[1024,1024]{1,0:T(8,128)} copy(f32[1024,1024]{0,1:T(8,128)} %broadcast_multiply_fusion) | data formatting | bytes 8388608 | tf_op jit(solution)/shard_map/mul | solution.py:31
  (1 shorter events, 0.0 us)
Async XLA Ops:
  6.5 39.6 %all-gather.5.cloned.1.call-start = ((), (), s32[]{:S(2)}) async-start(), calls=%async_computation.1 | async-start | bytes 5242880 | tf_op jit(solution)/shard_map/all_gather | solution.py:8
  7.3 115.6 %all-gather.3.cloned.1.call-start = ((), (), s32[]{:S(2)}) async-start(), calls=%async_computation | async-start | bytes 4718592 | tf_op jit(solution)/shard_map/all_gather | solution.py:21
Sparse Core Ops, SparseCore 0:
  8.9 37.1 all-gather.4
  48.1 74.6 all-gather.2
where the time goes:
time: 170 us
  waiting for transfers between devices  108 us (64%)
  blocking collectives  18.6 us (11%)
  between operations  13.4 us (8%)
  local copies, waits for them, and re-layouts  11.4 us (7%)
  matrix products  11.3 us (7%)
  other arithmetic  6.98 us (4%)
    all_gather x1, waiting for transfers between devices, per_device(): left_line = lax.all_gather(scaled_left, 'col', axis=1, tiled=True)  76.7 us
    all_gather x1, waiting for transfers between devices, taken_in(): lax.all_gather(a, axis, axis=dim, tiled=True)  30.7 us
    psum x1, blocking collectives, per_device(): row_power = lax.psum(jnp.sum(updated * updated, axis=1), 'col')  18.6 us
    dot_general x1, matrix products, join_panel(): jnp.dot(left_panel, right_panel, preferred_element_type=jnp.float32)  11.3 us
    unnamed x1, local copies, waits for them, and re-layouts  5.35 us
    mul x1, local copies, waits for them, and re-layouts, per_device(): updated * lax.rsqrt(row_power / (updated.shape[1] * lax.axis_size('col'))...  5.34 us
    mul x1, other arithmetic, per_device(): updated * lax.rsqrt(row_power / (updated.shape[1] * lax.axis_size('col'))...  4.98 us
  transfers between devices with their start and end apart: 2, of which 2 were waited for; matrix products, arithmetic and copies ran while one was open for 5% of the time, Pallas kernels for 0%

commit v1 on v0

--- a/solution.py
+++ b/solution.py
@@ -18,7 +18,8 @@
     part_scale = lax.dynamic_slice_in_dim(pivot_scale, lax.axis_index("col") * share, share)
     scaled_left = (left_factor.astype(jnp.float32) * part_scale).astype(jnp.bfloat16)
     begin = jnp.zeros((left_factor.shape[0], right_factor.shape[1]), jnp.float32)
-    left_line = lax.all_gather(scaled_left, "col", axis=1, tiled=True)
+    parts = lax.all_gather(scaled_left, "col", axis=0, tiled=False)
+    left_line = jnp.concatenate(parts, axis=1)
 
     def take_rows(carry, piece, start):
         left_piece = lax.dynamic_slice_in_dim(left_line, start, piece.shape[0], axis=1)

time: 170 us -> 170 us (level)
  waiting for transfers between devices: 108 us -> 98.4 us
  local copies, waits for them, and re-layouts: 11.4 us -> 17.9 us
  blocking collectives: 18.6 us -> 21.3 us
    all_gather x1, waiting for transfers between devices: 76.7 us -> 69.6 us  [per_device(): parts = lax.all_gather(scaled_left, 'col', axis=0, tiled=False)]
    reshape x0 -> x1, local copies, waits for them, and re-layouts: none -> 6.49 us  [per_device(): left_line = jnp.concatenate(parts, axis=1)]
    psum x1, blocking collectives: 18.6 us -> 21.3 us  [per_device(): row_power = lax.psum(jnp.sum(updated * updated, axis=1), 'col')]
    all_gather x1, waiting for transfers between devices: 30.7 us -> 28.1 us  [taken_in(): lax.all_gather(a, axis, axis=dim, tiled=True)]
  transfers between devices with their start and end apart: 2 -> 2, of which waited for: 2 -> 2; matrix products, arithmetic and copies ran while one was open for 5% -> 7% of each run, Pallas kernels for 0% -> 0%
where the time goes in v1:
time: 170 us; the launch traced here: 169 us
  waiting for transfers between devices  98.4 us (58%)
  blocking collectives  21.3 us (13%)
  local copies, waits for them, and re-layouts  17.9 us (11%)
  between operations  13.4 us (8%)
  matrix products  11.3 us (7%)
  other arithmetic  6.98 us (4%)
    all_gather x1, waiting for transfers between devices, per_device(): parts = lax.all_gather(scaled_left, 'col', axis=0, tiled=False)  69.6 us
    all_gather x1, waiting for transfers between devices, taken_in(): lax.all_gather(a, axis, axis=dim, tiled=True)  28.1 us
    psum x1, blocking collectives, per_device(): row_power = lax.psum(jnp.sum(updated * updated, axis=1), 'col')  21.3 us
    dot_general x1, matrix products, join_panel(): jnp.dot(left_panel, right_panel, preferred_element_type=jnp.float32)  11.3 us
    reshape x1, local copies, waits for them, and re-layouts, per_device(): left_line = jnp.concatenate(parts, axis=1)  6.49 us
    unnamed x1, local copies, waits for them, and re-layouts  5.35 us
    mul x1, local copies, waits for them, and re-layouts, per_device(): updated * lax.rsqrt(row_power / (updated.shape[1] * lax.axis_size('col'))...  5.34 us
    mul x1, other arithmetic, per_device(): updated * lax.rsqrt(row_power / (updated.shape[1] * lax.axis_size('col'))...  4.98 us
  transfers between devices with their start and end apart: 2, of which 2 were waited for; matrix products, arithmetic and copies ran while one was open for 7% of the time, Pallas kernels for 0%

profile of v1, /device:TPU:0, one launch (start us, length us, event | category | flops | bytes accessed | tf_op | source)
XLA Modules:
  0.0 169.4 jit_solution(16390551507384613821)
XLA Ops:
  6.5 0.0 all-gather.6.cloned.1.call-start
  6.5 0.8 dynamic_slice.3
  7.3 2.0 %multiply_convert_fusion = bf16[1024,256]{1,0:T(8,128)(2,1)} fusion(bf16[1024,256]{1,0:T(8,128)(2,1)} %param.4, f32[256]{0:T(256)S(1)} %dynamic_slice.3), kind=kLoop, calls=%fused_computation.3 | loop fusion | flops 786432 | bytes 1049600 | tf_op jit(solution)/shard_map/convert_element_type | solution.py:19
  9.3 0.0 all-gather.6.cloned.1.call-update
  9.3 0.0 all-gather.4.cloned.1.call-start
  9.4 0.7 all-gather.4.cloned.1.call-update
  10.1 5.3 %copy.10 = f32[1024,1024]{0,1:T(8,128)} copy(f32[1024,1024]{1,0:T(8,128)} %param.6) | data formatting | bytes 8388608 | tf_op args[2]
  15.4 69.6 %all-gather.6.cloned.1.call-done = bf16[8192,256]{1,0:T(8,128)(2,1)} async-done(((bf16[1024,256]{1,0:T(8,128)(2,1)}), bf16[8192,256]{1,0:T(8,128)(2,1)}) %all-gather.6.cloned.1.call-update) | async-done | bytes 4194320 | tf_op jit(solution)/shard_map/all_gather | solution.py:21
  85.0 6.5 %copy.9 = bf16[1024,8,256]{0,2,1:T(8,128)(2,1)} copy(bf16[1024,8,256]{2,0,1:T(8,128)(2,1)} %bitcast.6) | data formatting | bytes 8388608 | tf_op jit(solution)/shard_map/reshape | solution.py:22
  91.5 28.1 %all-gather.4.cloned.1.call-done = bf16[2048,1024]{1,0:T(8,128)(2,1)} async-done(((bf16[512,1024]{1,0:T(8,128)(2,1)}), bf16[2048,1024]{1,0:T(8,128)(2,1)}) %all-gather.4.cloned.1.call-update) | async-done | bytes 4194320 | tf_op jit(solution)/shard_map/all_gather | solution.py:8
  119.6 11.3 %multiply_reduce_fusion = (f32[1024]{0:T(1024)S(1)}, f32[1024,1024]{0,1:T(8,128)}) fusion(f32[1024,1024]{0,1:T(8,128)} %copy.10, bf16[1024,2048]{0,1:T(8,128)(2,1)} %bitcast.7, bf16[2048,1024]{1,0:T(8,128)(2,1)} %all-gather.4.cloned.1.call-done), kind=kOutput, calls=%fused_computation | convolution fusion | flops 4298112000 | bytes 16781312 | tf_op jit(solution)/shard_map/dot_general | solution.py:13
  130.9 21.3 %psum.7 = f32[1024]{0:T(1024)S(1)} all-reduce(f32[1024]{0:T(1024)S(1)} %get-tuple-element.5), channel_id=1, replica_groups=mesh['row'=4,'col'=8] {'col'}, use_global_device_ids=true, to_apply=%region_1.0 | all-reduce | flops 1024 | bytes 8192 | tf_op jit(solution)/shard_map/psum | solution.py:30
  152.3 5.0 %broadcast_multiply_fusion = f32[1024,1024]{0,1:T(8,128)} fusion(f32[1024,1024]{0,1:T(8,128)} %get-tuple-element.6, f32[1024]{0:T(1024)S(1)} %add_rsqrt_fusion), kind=kLoop, calls=%fused_computation.1 | loop fusion | flops 1048576 | bytes 8392704 | tf_op jit(solution)/shard_map/mul | solution.py:32
  157.2 5.3 %copy.11 = f32[1024,1024]{1,0:T(8,128)} copy(f32[1024,1024]{0,1:T(8,128)} %broadcast_multiply_fusion) | data formatting | bytes 8388608 | tf_op jit(solution)/shard_map/mul | solution.py:32
  (1 shorter events, 0.0 us)
Async XLA Ops:
  6.5 78.5 %all-gather.6.cloned.1.call-start = ((), (), s32[]{:S(2)}) async-start(), calls=%async_computation.1 | async-start | bytes 4718592 | tf_op jit(solution)/shard_map/all_gather | solution.py:21
  9.3 110.3 %all-gather.4.cloned.1.call-start = ((), (), s32[]{:S(2)}) async-start(), calls=%async_computation | async-start | bytes 5242880 | tf_op jit(solution)/shard_map/all_gather | solution.py:8
Sparse Core Ops, SparseCore 0:
  9.5 75.5 all-gather.5
  86.6 32.9 all-gather.3

commit v2 on v0

--- a/solution.py
+++ b/solution.py
@@ -26,7 +26,9 @@
 
     total = taken_in(right_factor, "row", 0, take_rows, begin)
     updated = matrix - total
-    row_power = lax.psum(jnp.sum(updated * updated, axis=1), "col")
+    block = jnp.sum(updated * updated, axis=1)
+    blocks = lax.all_gather(block, "col")
+    row_power = jnp.sum(blocks, axis=0)
     updated = (
         updated * lax.rsqrt(row_power / (updated.shape[1] * lax.axis_size("col")) + 1e-06)[:, None]
     )

time: 170 us -> 182 us (1.071)
  blocking collectives: 18.6 us -> 30.6 us
    all_gather x0 -> x1, blocking collectives: none -> 30.6 us  [per_device(): blocks = lax.all_gather(block, 'col')]
    psum x1 -> x0, blocking collectives: 18.6 us -> none  [per_device(): row_power = lax.psum(jnp.sum(updated * updated, axis=1), 'col')]
  transfers between devices with their start and end apart: 2 -> 2, of which waited for: 2 -> 2; matrix products, arithmetic and copies ran while one was open for 5% -> 4% of each run, Pallas kernels for 0% -> 0%
where the time goes in v2:
time: 182 us
  waiting for transfers between devices  108 us (59%)
  blocking collectives  30.6 us (17%)
  between operations  13.4 us (7%)
  local copies, waits for them, and re-layouts  11.5 us (6%)
  matrix products  11.3 us (6%)
  other arithmetic  6.99 us (4%)
    all_gather x1, waiting for transfers between devices, per_device(): left_line = lax.all_gather(scaled_left, 'col', axis=1, tiled=True)  76.7 us
    all_gather x1, waiting for transfers between devices, taken_in(): lax.all_gather(a, axis, axis=dim, tiled=True)  30.7 us
    all_gather x1, blocking collectives, per_device(): blocks = lax.all_gather(block, 'col')  30.6 us
    dot_general x1, matrix products, join_panel(): jnp.dot(left_panel, right_panel, preferred_element_type=jnp.float32)  11.3 us
    unnamed x1, local copies, waits for them, and re-layouts  5.35 us
    mul x1, local copies, waits for them, and re-layouts, per_device(): updated * lax.rsqrt(row_power / (updated.shape[1] * lax.axis_size('col'))...  5.34 us
    mul x1, other arithmetic, per_device(): updated * lax.rsqrt(row_power / (updated.shape[1] * lax.axis_size('col'))...  4.98 us
  transfers between devices with their start and end apart: 2, of which 2 were waited for; matrix products, arithmetic and copies ran while one was open for 4% of the time, Pallas kernels for 0%

profile of v2, /device:TPU:0, one launch (start us, length us, event | category | flops | bytes accessed | tf_op | source)
XLA Modules:
  0.0 181.9 jit_solution(1931856246170519597)
XLA Ops:
  6.5 0.0 all-gather.6.cloned.1.call-start
  6.5 0.7 all-gather.6.cloned.1.call-update
  7.3 0.0 all-gather.4.cloned.1.call-start
  7.3 0.8 dynamic_slice.3
  8.1 2.0 %multiply_convert_fusion = bf16[1024,256]{1,0:T(8,128)(2,1)} fusion(bf16[1024,256]{1,0:T(8,128)(2,1)} %param.4, f32[256]{0:T(256)S(1)} %dynamic_slice.3), kind=kLoop, calls=%fused_computation.3 | loop fusion | flops 786432 | bytes 1049600 | tf_op jit(solution)/shard_map/convert_element_type | solution.py:19
  10.1 0.0 all-gather.4.cloned.1.call-update
  10.1 5.3 %copy.9 = f32[1024,1024]{0,1:T(8,128)} copy(f32[1024,1024]{1,0:T(8,128)} %param.6) | data formatting | bytes 8388608 | tf_op args[2]
  15.4 30.7 %all-gather.6.cloned.1.call-done = bf16[2048,1024]{1,0:T(8,128)(2,1)} async-done(((bf16[512,1024]{1,0:T(8,128)(2,1)}), bf16[2048,1024]{1,0:T(8,128)(2,1)}) %all-gather.6.cloned.1.call-update) | async-done | bytes 4194320 | tf_op jit(solution)/shard_map/all_gather | solution.py:8
  46.1 76.7 %all-gather.4.cloned.1.call-done = bf16[1024,2048]{1,0:T(8,128)(2,1)} async-done(((bf16[1024,256]{1,0:T(8,128)(2,1)}), bf16[1024,2048]{1,0:T(8,128)(2,1)}) %all-gather.4.cloned.1.call-update) | async-done | bytes 4194320 | tf_op jit(solution)/shard_map/all_gather | solution.py:21
  122.8 11.3 %multiply_reduce_fusion = (f32[1024]{0:T(1024)S(1)}, f32[1024,1024]{0,1:T(8,128)}) fusion(f32[1024,1024]{0,1:T(8,128)} %copy.9, bf16[1024,2048]{1,0:T(8,128)(2,1)} %all-gather.4.cloned.1.call-done, bf16[2048,1024]{1,0:T(8,128)(2,1)} %all-gather.6.cloned.1.call-done), kind=kOutput, calls=%fused_computation | convolution fusion | flops 4298112000 | bytes 16781312 | tf_op jit(solution)/shard_map/dot_general | solution.py:13
  134.1 30.6 %all-gather = f32[8192]{0:T(1024)S(1)} all-gather(f32[1024]{0:T(1024)S(1)} %get-tuple-element.5), channel_id=2, replica_groups=mesh['row'=4,'col'=8] {'col'}, dimensions={0}, use_global_device_ids=true | all-gather | bytes 36864 | tf_op jit(solution)/shard_map/all_gather | solution.py:30
  164.8 5.0 %broadcast_multiply_fusion = f32[1024,1024]{0,1:T(8,128)} fusion(f32[1024,1024]{0,1:T(8,128)} %get-tuple-element.6, f32[1024]{0:T(1024)S(1)} %add_rsqrt_fusion), kind=kLoop, calls=%fused_computation.1 | loop fusion | flops 1048576 | bytes 8392704 | tf_op jit(solution)/shard_map/mul | solution.py:33
  169.8 5.3 %copy.10 = f32[1024,1024]{1,0:T(8,128)} copy(f32[1024,1024]{0,1:T(8,128)} %broadcast_multiply_fusion) | data formatting | bytes 8388608 | tf_op jit(solution)/shard_map/mul | solution.py:33
  (3 shorter events, 0.0 us)
Async XLA Ops:
  6.5 39.6 %all-gather.6.cloned.1.call-start = ((), (), s32[]{:S(2)}) async-start(), calls=%async_computation.1 | async-start | bytes 5242880 | tf_op jit(solution)/shard_map/all_gather | solution.py:8
  7.3 115.6 %all-gather.4.cloned.1.call-start = ((), (), s32[]{:S(2)}) async-start(), calls=%async_computation | async-start | bytes 4718592 | tf_op jit(solution)/shard_map/all_gather | solution.py:21
Sparse Core Ops, SparseCore 0:
  8.9 37.1 all-gather.5
  48.1 74.6 all-gather.3
